TPU v7x, 32 devices: a whole 2x2x4 slice. The times are simulated.
32 devices in a mesh: head: 8 (over z, x), client: 4 (over y, core).
Axes of the slice: x: 2, y: 2, z: 4, core: 2. Of those that a mesh axis runs over, the one named last changes fastest.
Arguments:
- client_ids: int32 [32], replicated, may hold values from 0 to 127, as said below
- client_table: bfloat16 [128, 256], replicated, may hold values from -6 to 6
- in_weight: bfloat16 [256, 4096], P(None, 'client'), may hold values from -0.375 to 0.375
- in_bias: float32 [4096], P('client'), may hold values from -3 to 3
- head_weight: bfloat16 [4096, 131072], P('client', 'head'), may hold values from -0.09375 to 0.09375
- tokens: int32 [32, 256], P(('head', 'client')), may hold values from 0 to 255
- labels: int32 [32, 256], P(('head', 'client')), may hold values from 0 to 255
- byte_table: bfloat16 [256, 4096], P(None, 'client'), may hold values from -5.5 to 6.7
- out_table: bfloat16 [256, 4096], P(None, 'client'), may hold values from -5.625 to 5.625
Outputs:
- head_grad: bfloat16 [4096, 131072], P('client', 'head')
- in_grad: float32 [256, 4096], P(None, 'client')
- losses: float32 [32], P(('head', 'client'))
Inputs may be any that keep to these rules, and one draw needn't show every extreme that they name: `client_ids`: distinct population indices.
All inputs are finite; a program needn't handle non-finite values.
Results may differ from a plain program's by a relative error of at most 0.0085.
Values may be sent and summed in bfloat16 or wider, within the bound.
A program may use at most 128 MiB of HBM per device.

v0:
```python
import jax
import jax.numpy as jnp
from jax import lax
from jax.sharding import PartitionSpec as P

EPSILON = 1e-06
learn_rate = 0.1


def client_loss(factor_a, factor_b, inputs, label_row, out_table):
    depth = factor_a.shape[0]
    rank_size = factor_a.shape[1]
    normed_in = inputs * lax.rsqrt(jnp.mean(inputs * inputs, -1, keepdims=True) + EPSILON)
    low_rank = jnp.dot(normed_in, factor_a, precision=lax.Precision.HIGHEST)
    adapted = inputs + jnp.dot(low_rank, factor_b, precision=lax.Precision.HIGHEST) / jnp.sqrt(
        jnp.float32(depth * rank_size)
    )
    normed = (adapted * lax.rsqrt(jnp.mean(adapted * adapted, -1, keepdims=True) + EPSILON)).astype(
        jnp.bfloat16
    )
    logits = lax.dot_general(
        normed, out_table, (((1,), (1,)), ((), ())), preferred_element_type=jnp.float32
    )
    logits = logits * (4.0 / jnp.sqrt(jnp.float32(depth)))
    log_total = jax.nn.logsumexp(logits, -1)
    vocab_ids = lax.broadcasted_iota(jnp.int32, logits.shape, 1)
    picked = jnp.sum(jnp.where(vocab_ids == label_row[:, None], logits, 0.0), -1)
    return jnp.sum(log_total - picked)


def train_client(factor_row, token_row, label_row, byte_table, out_table):
    depth = byte_table.shape[1]
    split_at = factor_row.shape[0] // 2
    rank_size = split_at // depth
    start_a = factor_row[:split_at].reshape(depth, rank_size).astype(jnp.float32)
    start_b = factor_row[split_at:].reshape(rank_size, depth).astype(jnp.float32)
    onehot = (
        token_row[:, None]
        == lax.broadcasted_iota(jnp.int32, (token_row.shape[0], byte_table.shape[0]), 1)
    ).astype(jnp.bfloat16)
    inputs = jnp.dot(onehot, byte_table, preferred_element_type=jnp.float32)
    loss_grad = jax.value_and_grad(client_loss, argnums=(0, 1))
    first_loss, (grad_a, grad_b) = loss_grad(start_a, start_b, inputs, label_row, out_table)
    middle_a = start_a - learn_rate * grad_a
    middle_b = start_b - learn_rate * grad_b
    second_loss, (grad_a, grad_b) = loss_grad(middle_a, middle_b, inputs, label_row, out_table)
    final_a = middle_a - learn_rate * grad_a
    final_b = middle_b - learn_rate * grad_b
    deltas = jnp.concatenate(
        [(final_a - start_a).reshape(-1), (final_b - start_b).reshape(-1)]
    ).astype(jnp.bfloat16)
    return (deltas, first_loss / token_row.shape[0])


def local(
    client_ids, client_table, in_weight, in_bias, head_weight, tokens, labels, byte_table, out_table
):
    head_count = lax.axis_size("head")
    group_count = lax.axis_size("client")
    per_device = tokens.shape[0]
    byte_full, out_full = (
        lax.all_gather(byte_table, "client", axis=1, tiled=True),
        lax.all_gather(out_table, "client", axis=1, tiled=True),
    )
    ordered = client_ids.reshape(head_count, group_count, per_device).transpose(1, 0, 2).reshape(-1)
    chosen = client_table[ordered]
    preact = jnp.dot(chosen, in_weight, preferred_element_type=jnp.float32) + in_bias
    hidden = jnp.maximum(preact, 0.0).astype(jnp.bfloat16)
    hidden_rows = hidden
    summed = lax.psum_scatter(
        jnp.dot(hidden_rows, head_weight, preferred_element_type=jnp.float32),
        "client",
        scatter_dimension=0,
        tiled=True,
    )
    owned = lax.all_to_all(
        summed.astype(jnp.bfloat16), "head", split_axis=0, concat_axis=1, tiled=True
    )

    def run_client(record):
        return train_client(record[0], record[1], record[2], byte_full, out_full)

    deltas, losses = lax.map(run_client, (owned, tokens, labels))
    returned = lax.all_to_all(deltas, "head", split_axis=1, concat_axis=0, tiled=True)
    received = lax.all_gather(returned, "client", axis=0, tiled=True)
    hidden_rows = hidden
    grad_sum = lax.dot_general(
        hidden_rows, received, (((0,), (0,)), ((), ())), preferred_element_type=jnp.float32
    )
    partial_value = lax.dot_general(
        received, head_weight, (((1,), (1,)), ((), ())), preferred_element_type=jnp.float32
    )
    hidden_back = partial_value
    grad_sum, hidden_back = (grad_sum, hidden_back)
    hidden_back = lax.psum(hidden_back, "head")
    masked = jnp.where(preact > 0, hidden_back, 0.0)
    in_grad = lax.dot_general(
        chosen.astype(jnp.float32),
        masked,
        (((0,), (0,)), ((), ())),
        precision=lax.Precision.HIGHEST,
    )
    return (grad_sum.astype(jnp.bfloat16), in_grad, losses)


def solution(mesh):
    placed = (
        P(),
        P(),
        P(None, "client"),
        P("client"),
        P("client", "head"),
        P(("head", "client"), None),
        P(("head", "client"), None),
        P(None, "client"),
        P(None, "client"),
    )
    return jax.shard_map(
        local,
        mesh=mesh,
        in_specs=placed,
        out_specs=(P("client", "head"), P(None, "client"), P(("head", "client"))),
        check_vma=False,
    )
```

profile of v0, /device:TPU:0, one launch (start us, length us, event | category | flops | bytes accessed | tf_op | source)
XLA Modules:
  0.0 274.2 jit_solution(7337150185194927193)
XLA Ops:
  10.5 14.9 %fusion.59 = f32[32,16384]{1,0:T(8,128)} fusion(bf16[1024,16384]{1,0:T(8,128)(2,1)} %param.13, f32[32,1024]{1,0:T(8,128)S(1)} %convolution_add_fusion), kind=kOutput, calls=%fused_computation.91 | convolution fusion | flops 1073807360 | bytes 35782656 | tf_op jit(solution)/shard_map/dot_general | solution.py:71
  26.9 32.6 %reduce-scatter.2.cloned.1.call-done = f32[8,16384]{1,0:T(8,128)} async-done(((f32[32,16384]{1,0:T(8,128)}), f32[8,16384]{1,0:T(8,128)}) %reduce-scatter.2.cloned.1.call-update) | async-done | bytes 524304 | tf_op jit(solution)/shard_map/reduce_scatter | solution.py:70
  62.8 5.5 %all-to-all-start = ((bf16[8,2,8192]{2,1,0:T(2,128)(2,1)}), bf16[8,2,8192]{2,1,0:T(2,128)(2,1)S(1)}, u32[]{:S(2)}, u32[]{:S(2)}) async-start(bf16[8,2,8192]{2,1,0:T(2,128)(2,1)} %reshape.181), calls=%async_computation.1 | async-start | bytes 524288 | tf_op jit(solution)/shard_map/all_to_all | solution.py:76
  68.3 15.3 %all-gather.5.cloned.1.call-done = bf16[256,4096]{1,0:T(8,128)(2,1)} async-done(((bf16[256,1024]{1,0:T(8,128)(2,1)}), bf16[256,4096]{1,0:T(8,128)(2,1)}) %all-gather.5.cloned.1.call-update) | async-done | bytes 2097168 | tf_op jit(solution)/shard_map/all_gather | solution.py:62
  83.7 4.4 %multiply_reduce_fusion.2 = (f32[256]{0:T(256)S(1)}, f32[256,4096]{1,0:T(8,128)}) fusion(bf16[256,4096]{1,0:T(8,128)(2,1)} %all-gather.5.cloned.1.call-done, s32[256]{0:T(256)S(1)} %bitcast.43), kind=kOutput, calls=%fused_computation.34 | convolution fusion | flops 539033344 | bytes 6293504 | tf_op jit(solution)/shard_map/while/body/eval_jaxpr/dot_general | solution.py:41
  90.9 4.8 %fusion.18 = f32[256,16]{0,1:T(8,128)S(1)} fusion(bf16[4096,16]{1,0:T(8,128)(2,1)S(1)} %reshape.168, f32[256,4096]{1,0:T(8,128)} %get-tuple-element.34, f32[256]{0:T(256)S(1)} %add_rsqrt_fusion), kind=kOutput, calls=%fused_computation.39 | convolution fusion | flops 202375168 | bytes 4342784 | tf_op jit(solution)/shard_map/while/body/eval_jaxpr/jvp()/dot_general | solution.py:14
  95.7 4.3 %multiply_reduce_fusion.1 = (f32[256]{0:T(256)S(1)}, f32[256,4096]{1,0:T(8,128)}) fusion(f32[256,4096]{1,0:T(8,128)S(1)} %copy-done.2, f32[256,16]{0,1:T(8,128)S(1)} %fusion.18, bf16[16,4096]{1,0:T(8,128)(2,1)S(1)} %reshape.169), kind=kOutput, calls=%fused_computation.33 | convolution fusion | flops 205520640 | bytes 8537088 | tf_op jit(solution)/shard_map/while/body/eval_jaxpr/jvp()/dot_general | solution.py:15
  100.0 7.8 %all-gather.7.cloned.1.call-done = bf16[256,4096]{1,0:T(8,128)(2,1)} async-done(((bf16[256,1024]{1,0:T(8,128)(2,1)}), bf16[256,4096]{1,0:T(8,128)(2,1)}) %all-gather.7.cloned.1.call-update) | async-done | bytes 2097168 | tf_op jit(solution)/shard_map/all_gather | solution.py:63
  107.8 3.8 %fusion.78 = (f32[256]{0:T(256)S(1)}, f32[256,256]{0,1:T(8,128)S(1)}) fusion(bf16[256,4096]{1,0:T(8,128)(2,1)} %all-gather.7.cloned.1.call-done, f32[256,4096]{1,0:T(8,128)} %get-tuple-element.36, f32[256]{0:T(256)S(1)} %fusion.60), kind=kOutput, calls=%fused_computation.118 | convolution fusion | flops 539098880 | bytes 6555648 | tf_op jit(solution)/shard_map/while/body/eval_jaxpr/jvp()/dot_general | solution.py:21
  113.5 2.8 %fusion.76 = f32[256,16]{0,1:T(8,128)S(1)} fusion(bf16[16,4096]{1,0:T(8,128)(2,1)S(1)} %reshape.169, bf16[256,4096]{1,0:T(8,128)(2,1)S(1)} %get-tuple-element.40, f32[256,4096]{1,0:T(8,128)S(1)} %copy-done.4, f32[256]{0:T(256)S(1)} %multiply_multiply_fusion.1, f32[256]{0:T(256)S(1)} %fusion.60), kind=kOutput, calls=%fused_computation.117 | convolution fusion | flops 207618048 | bytes 6440960 | tf_op jit(solution)/shard_map/while/body/eval_jaxpr/transpose(jvp())/dot_general | solution.py:15
  116.3 3.1 %fusion.6 = f32[16,4096]{1,0:T(8,128)S(1)} fusion(f32[256,16]{0,1:T(8,128)S(1)} %fusion.18, bf16[16,4096]{1,0:T(8,128)(2,1)S(1)} %reshape.169, bf16[256,4096]{1,0:T(8,128)(2,1)S(1)} %get-tuple-element.40, f32[256,4096]{1,0:T(8,128)S(1)} %copy-done.4, f32[256]{0:T(256)S(1)} %multiply_multiply_fusion.1, f32[256]{0:T(256)S(1)} %fusion.60), kind=kOutput, calls=%fused_computation.21 | convolution fusion | flops 207814656 | bytes 6703104 | tf_op jit(solution)/shard_map/while/body/eval_jaxpr/transpose(jvp())/dot_general | solution.py:15
  119.5 2.5 fusion.7
  122.0 3.4 %fusion.15 = f32[256,16]{0,1:T(8,128)S(1)} fusion(f32[4096,16]{0,1:T(8,128)S(1)} %fusion.7, f32[256,4096]{1,0:T(8,128)S(1)} %copy-done.3, f32[256]{0:T(256)S(1)} %add_rsqrt_fusion), kind=kOutput, calls=%fused_computation.36 | convolution fusion | flops 202375168 | bytes 4473856 | tf_op jit(solution)/shard_map/while/body/eval_jaxpr/jvp()/dot_general | solution.py:14
  125.4 4.1 %multiply_reduce_fusion = (f32[256]{0:T(256)S(1)}, f32[256,4096]{1,0:T(8,128)S(1)}) fusion(f32[256,4096]{1,0:T(8,128)S(1)} %copy-done.3, f32[256,16]{0,1:T(8,128)S(1)} %fusion.15, f32[16,4096]{1,0:T(8,128)S(1)} %fusion.6), kind=kOutput, calls=%fused_computation.31 | convolution fusion | flops 205520640 | bytes 8668160 | tf_op jit(solution)/shard_map/while/body/eval_jaxpr/jvp()/dot_general | solution.py:15
  131.4 4.4 %fusion.73 = f32[256,16]{0,1:T(8,128)S(1)} fusion(f32[16,4096]{1,0:T(8,128)S(1)} %fusion.6, bf16[256,4096]{1,0:T(8,128)(2,1)S(1)} %get-tuple-element.46, f32[256,4096]{1,0:T(8,128)S(1)} %get-tuple-element.42, f32[256]{0:T(256)S(1)} %multiply_multiply_fusion, f32[256]{0:T(256)S(1)} %fusion.61), kind=kOutput, calls=%fused_computation.116 | convolution fusion | flops 207618048 | bytes 6572032 | tf_op jit(solution)/shard_map/while/body/eval_jaxpr/transpose(jvp())/dot_general | solution.py:15
  135.8 2.9 %fusion.9 = bf16[16,4096]{1,0:T(8,128)(2,1)S(1)} fusion(f32[16,4096]{1,0:T(8,128)S(1)} %fusion.6, f32[256,16]{0,1:T(8,128)S(1)} %fusion.15, bf16[16,4096]{1,0:T(8,128)(2,1)S(1)} %reshape.169, bf16[256,4096]{1,0:T(8,128)(2,1)S(1)} %get-tuple-element.46, f32[256,4096]{1,0:T(8,128)S(1)} %get-tuple-element.42, f32[256]{0:T(256)S(1)} %multiply_multiply_fusion, ...), kind=kOutput, calls=%fused_computation.25 | convolution fusion | flops 207945728 | bytes 6834176 | tf_op jit(solution)/shard_map/while/body/eval_jaxpr/transpose(jvp())/dot_general | solution.py:15
  138.8 2.5 fusion.8
  143.7 2.2 reduce.5
  146.1 14.8 %all_to_all.26 = bf16[8,2,8192]{2,1,0:T(2,128)(2,1)S(1)} all-to-all(bf16[8,2,8192]{2,1,0:T(2,128)(2,1)S(1)} %reshape.183), channel_id=1, replica_groups=mesh['head'=8,'client'=4] {'head'}, dimensions={0} | all-to-all | bytes 524288 | tf_op jit(solution)/shard_map/all_to_all | solution.py:84
  162.8 14.3 %all-gather.9.cloned.1.call-done = bf16[1,32,16384]{2,1,0:T(8,128)(2,1)} async-done(((bf16[1,8,16384]{2,1,0:T(8,128)(2,1)}), bf16[1,32,16384]{2,1,0:T(8,128)(2,1)}) %all-gather.9.cloned.1.call-update) | async-done | bytes 1048592 | tf_op jit(solution)/shard_map/all_gather | solution.py:85
  177.1 16.1 %fusion.30 = f32[32,1024]{1,0:T(8,128)} fusion(bf16[1024,16384]{1,0:T(8,128)(2,1)} %param.13, bf16[1,32,16384]{2,1,0:T(8,128)(2,1)} %all-gather.9.cloned.1.call-done), kind=kOutput, calls=%fused_computation.52 | convolution fusion | flops 1073741824 | bytes 34734080 | tf_op jit(solution)/shard_map/dot_general | solution.py:90
  193.2 14.9 %convolution_convert_fusion = bf16[1024,16384]{1,0:T(8,128)(2,1)} fusion(bf16[1,32,16384]{2,1,0:T(8,128)(2,1)S(1)} %copy-done.6, f32[32,1024]{1,0:T(8,128)S(1)} %convolution_add_fusion), kind=kOutput, calls=%fused_computation.1 | convolution fusion | flops 1090584576 | bytes 34734080 | tf_op jit(solution)/shard_map/dot_general | solution.py:87
  208.1 55.7 %all-reduce.2.cloned.1.call-done = f32[32,1024]{1,0:T(8,128)} async-done(((f32[32,1024]{1,0:T(8,128)}), f32[32,1024]{1,0:T(8,128)}) %all-reduce.2.cloned.1.call-update) | async-done | bytes 131088 | tf_op jit(solution)/shard_map/psum | solution.py:95
  263.8 2.5 fusion.42
  (67 shorter events, 18.5 us)
Async XLA Ops:
  7.2 2.5 copy-start
  7.2 52.3 %reduce-scatter.2.cloned.1.call-start = ((), (), s32[]{:S(2)}) async-start(), calls=%async_computation.3 | async-start | bytes 2621440 | tf_op jit(solution)/shard_map/reduce_scatter | solution.py:70
  25.4 58.2 %copy-start.7 = (s32[1,256]{1,0:T(1,128)S(1)}, s32[1,256]{1,0:T(1,128)}, u32[]{:S(2)}) copy-start(s32[1,256]{1,0:T(1,128)} %param.14) | copy-start | bytes 3076
  25.4 58.2 %all-gather.5.cloned.1.call-start = ((), (), s32[]{:S(2)}) async-start(), calls=%async_computation.4 | async-start | bytes 2621440 | tf_op jit(solution)/shard_map/all_gather | solution.py:62
  26.2 81.6 %all-gather.7.cloned.1.call-start = ((), (), s32[]{:S(2)}) async-start(), calls=%async_computation.5 | async-start | bytes 2621440 | tf_op jit(solution)/shard_map/all_gather | solution.py:63
  62.8 25.2 %all-to-all-start = ((bf16[8,2,8192]{2,1,0:T(2,128)(2,1)}), bf16[8,2,8192]{2,1,0:T(2,128)(2,1)S(1)}, u32[]{:S(2)}, u32[]{:S(2)}) async-start(bf16[8,2,8192]{2,1,0:T(2,128)(2,1)} %reshape.181), calls=%async_computation.1 | async-start | bytes 524288 | tf_op jit(solution)/shard_map/all_to_all | solution.py:76
  68.3 108.8 %all-gather.9.cloned.1.call-start = ((), (), s32[]{:S(2)}) async-start(), calls=%async_computation.7 | async-start | bytes 1310720 | tf_op jit(solution)/shard_map/all_gather | solution.py:85
  90.9 4.9 %copy-start.2 = (f32[256,4096]{1,0:T(8,128)S(1)}, f32[256,4096]{1,0:T(8,128)}, u32[]{:S(2)}) copy-start(f32[256,4096]{1,0:T(8,128)} %get-tuple-element.34) | copy-start | bytes 12582916
  100.0 11.7 %copy-start.8 = (s32[1,256]{1,0:T(1,128)S(1)}, s32[1,256]{1,0:T(1,128)}, u32[]{:S(2)}) copy-start(s32[1,256]{1,0:T(1,128)} %param.15) | copy-start | bytes 3076
  107.8 4.6 %copy-start.4 = (f32[256,4096]{1,0:T(8,128)S(1)}, f32[256,4096]{1,0:T(8,128)}, u32[]{:S(2)}) copy-start(f32[256,4096]{1,0:T(8,128)} %get-tuple-element.36) | copy-start | bytes 12582916
  107.8 4.7 %copy-start.5 = (bf16[256,4096]{1,0:T(8,128)(2,1)S(1)}, bf16[256,4096]{1,0:T(8,128)(2,1)}, u32[]{:S(2)}) copy-start(bf16[256,4096]{1,0:T(8,128)(2,1)} %all-gather.7.cloned.1.call-done) | copy-start | bytes 6291460
  116.3 3.2 %copy-start.3 = (f32[256,4096]{1,0:T(8,128)S(1)}, f32[256,4096]{1,0:T(8,128)}, u32[]{:S(2)}) copy-start(f32[256,4096]{1,0:T(8,128)} %get-tuple-element.34) | copy-start | bytes 12582916
  162.2 101.7 %all-reduce.2.cloned.1.call-start = ((), (), s32[]{:S(2)}) async-start(), calls=%async_computation.6 | async-start | bytes 262144 | tf_op jit(solution)/shard_map/psum | solution.py:95
  177.1 16.1 %copy-start.6 = (bf16[1,32,16384]{2,1,0:T(8,128)(2,1)S(1)}, bf16[1,32,16384]{2,1,0:T(8,128)(2,1)}, u32[]{:S(2)}) copy-start(bf16[1,32,16384]{2,1,0:T(8,128)(2,1)} %all-gather.9.cloned.1.call-done) | copy-start | bytes 3145732
  193.2 73.1 %copy-start.1 = (bf16[256,1024]{1,0:T(8,128)(2,1)S(1)}, bf16[256,1024]{1,0:T(8,128)(2,1)}, u32[]{:S(2)}) copy-start(bf16[256,1024]{1,0:T(8,128)(2,1)} %param.11) | copy-start | bytes 1572868
Sparse Core Ops, SparseCore 0:
  25.6 33.9 reduce-scatter.1
  61.1 22.5 all-gather.4
  85.2 22.5 all-gather.6
  162.3 14.7 all-gather.8
  193.3 70.4 all-reduce.1
where the time goes:
time: 278 us; the launch traced here: 274 us
  waiting for transfers between devices  127 us (46%)
  matrix products  95.1 us (34%)
  between operations  15.9 us (6%)
  blocking collectives  14.8 us (5%)
  local copies, waits for them, and re-layouts  10.5 us (4%)
  starting transfers between devices  5.69 us (2%)
  other arithmetic  5.08 us (2%)
    psum x1, waiting for transfers between devices, local(): hidden_back = lax.psum(hidden_back, 'head')  55.7 us
    reduce_scatter x1, waiting for transfers between devices, local(): lax.psum_scatter(jnp.dot(hidden_rows, head_weight, preferred_element_type...  32.6 us
    dot_general x6, matrix products, client_loss(): jnp.dot(low_rank, factor_b, precision=lax.Precision.HIGHEST)  21.7 us
    dot_general x1, matrix products, local(): lax.dot_general(received, head_weight, (((1,), (1,)), ((), ())), preferre...  16.1 us
    all_gather x1, waiting for transfers between devices, local(): lax.all_gather(byte_table, 'client', axis=1, tiled=True)  15.3 us
    dot_general x1, matrix products, local(): lax.dot_general(hidden_rows, received, (((0,), (0,)), ((), ())), preferre...  14.9 us
    dot_general x1, matrix products, local(): jnp.dot(hidden_rows, head_weight, preferred_element_type=jnp.float32)  14.9 us
    all_to_all x1, blocking collectives, local(): lax.all_to_all(deltas, 'head', split_axis=1, concat_axis=0, tiled=True)  14.8 us
  transfers between devices with their start and end apart: 6, of which 5 were waited for; matrix products, arithmetic and copies ran while one was open for 13% of the time, Pallas kernels for 0%

commit v1 on v0

v1 whole, which is shorter than its diff:
```python
import jax
import jax.numpy as jnp
from jax import lax
from jax.sharding import PartitionSpec as P

EPSILON = 1e-06
learn_rate = 0.1


FULL = lax.Precision.HIGHEST


def mm(x, y, over_x=1, over_y=0):
    return lax.dot_general(
        x, y, (((over_x,), (over_y,)), ((), ())), precision=FULL, preferred_element_type=jnp.float32
    )


def exact(x, y, over_x, over_y):
    return lax.dot_general(
        x, y, (((over_x,), (over_y,)), ((), ())), preferred_element_type=jnp.float32
    )


def halves(x):
    top = lax.reduce_precision(x, 8, 7)
    rest = x - top
    return jnp.concatenate([top.astype(jnp.bfloat16), rest.astype(jnp.bfloat16)], 1)


def inner_step(u, n_in, m_out, k_bb, gram_io, mean_in, pair_count, depth, scale):
    uk = mm(u, k_bb)
    z = gram_io + scale * mm(u, m_out, 1, 1)
    q = mean_in + jnp.sum(u * (2.0 * scale * n_in + (scale * scale) * uk), -1, keepdims=True) / depth
    r = lax.rsqrt(q + EPSILON)
    kappa = 4.0 / jnp.sqrt(jnp.float32(depth))
    logits = (kappa * r) * z
    top = jnp.max(logits, -1, keepdims=True)
    raised = jnp.exp(logits - top)
    total = jnp.sum(raised, -1, keepdims=True)
    row_count = jnp.sum(pair_count, -1, keepdims=True)
    loss = jnp.sum(row_count * (jnp.log(total) + top)) - jnp.sum(pair_count * logits)
    slope = row_count * (raised / total) - pair_count
    dz = (kappa * r) * slope
    dr = kappa * jnp.sum(slope * z, -1, keepdims=True)
    e = dr * (-1.0 / depth) * (r * r * r)
    gu = scale * (mm(dz, m_out) + e * (n_in + scale * uk))
    w = mm(dz, u, 0, 0)
    x = e * u
    y = mm(u, x, 0, 0)
    return loss, gu, w, x, y


def table_products(byte_full, out_full):
    depth = byte_full.shape[1]
    gram_ii = exact(byte_full, byte_full, 1, 1)
    gram_io = exact(byte_full, out_full, 1, 1)
    gram_oo = exact(out_full, out_full, 1, 1)
    size = gram_ii.shape[0]
    diagonal = lax.broadcasted_iota(jnp.int32, (size, size), 0) == lax.broadcasted_iota(
        jnp.int32, (size, size), 1
    )
    mean_in = jnp.sum(jnp.where(diagonal, gram_ii, 0.0), -1, keepdims=True) / depth
    return gram_ii, gram_io, gram_oo, mean_in


def train_client(factor_row, token_row, label_row, byte_full, out_full, products):
    gram_ii, gram_io, gram_oo, mean_in = products
    vocab, depth = byte_full.shape
    split_at = factor_row.shape[0] // 2
    rank = split_at // depth
    scale = 1.0 / jnp.sqrt(jnp.float32(depth * rank))
    a0 = factor_row[:split_at].reshape(depth, rank)
    b0 = factor_row[split_at:].reshape(rank, depth)
    ids = lax.broadcasted_iota(jnp.int32, (vocab, token_row.shape[0]), 0)
    pair_count = exact(
        (ids == token_row[None, :]).astype(jnp.bfloat16),
        (ids == label_row[None, :]).astype(jnp.bfloat16),
        1,
        1,
    )
    rn = lax.rsqrt(mean_in + EPSILON)
    u0 = rn * exact(byte_full, a0, 1, 0)
    n0 = exact(byte_full, b0, 1, 1)
    m0 = exact(out_full, b0, 1, 1)
    k0 = exact(b0, b0, 1, 1)
    fixed = (gram_io, mean_in, pair_count, depth, scale)
    first_loss, gu0, w0, x0, y0 = inner_step(u0, n0, m0, k0, *fixed)
    rate = learn_rate * scale
    w0, x0, y0 = -rate * w0, -rate * x0, (-rate * scale) * y0
    u1 = u0 - learn_rate * rn * mm(gram_ii, rn * gu0)
    n1 = n0 + mm(gram_io, w0) + mm(gram_ii, x0) + mm(n0, y0)
    m1 = m0 + mm(gram_oo, w0) + mm(gram_io, x0, 0, 0) + mm(m0, y0)
    cross = k0 + mm(y0, k0, 0, 0) + mm(w0, m0, 0, 0) + mm(x0, n0, 0, 0)
    k1 = cross + mm(cross, y0) + mm(m1, w0, 0, 0) + mm(n1, x0, 0, 0)
    _, gu1, w1, x1, y1 = inner_step(u1, n1, m1, k1, *fixed)
    w1, x1, y1 = -rate * w1, -rate * x1, (-rate * scale) * y1
    ga = (-learn_rate) * rn * (gu0 + gu1)
    wf = w0 + w1 + mm(w0, y1)
    xf = x0 + x1 + mm(x0, y1)
    yf = y0 + y1 + mm(y0, y1)
    da = exact(byte_full, halves(ga), 0, 0)
    da = da[:, :rank] + da[:, rank:]
    db = (
        exact(halves(wf), out_full, 0, 0)
        + exact(halves(xf), byte_full, 0, 0)
        + exact(halves(yf), b0, 0, 0)
    )
    db = db[:rank] + db[rank:]
    deltas = jnp.concatenate([da.astype(jnp.bfloat16).reshape(-1), db.astype(jnp.bfloat16).reshape(-1)])
    return deltas, first_loss / token_row.shape[0]


def local(
    client_ids, client_table, in_weight, in_bias, head_weight, tokens, labels, byte_table, out_table
):
    head_count = lax.axis_size("head")
    group_count = lax.axis_size("client")
    per_device = tokens.shape[0]
    byte_full, out_full = (
        lax.all_gather(byte_table, "client", axis=1, tiled=True),
        lax.all_gather(out_table, "client", axis=1, tiled=True),
    )
    products = table_products(byte_full, out_full)
    ordered = client_ids.reshape(head_count, group_count, per_device).transpose(1, 0, 2).reshape(-1)
    chosen = client_table[ordered]
    preact = jnp.dot(chosen, in_weight, preferred_element_type=jnp.float32) + in_bias
    hidden = jnp.maximum(preact, 0.0).astype(jnp.bfloat16)
    partial = jnp.dot(hidden, head_weight, preferred_element_type=jnp.float32).astype(jnp.bfloat16)
    rows, columns = partial.shape
    parts = lax.all_to_all(
        partial.reshape(group_count, rows // group_count, columns), "client", split_axis=0, concat_axis=0
    )
    summed = jnp.sum(parts.astype(jnp.float32), 0)
    owned = lax.all_to_all(
        summed.astype(jnp.bfloat16), "head", split_axis=0, concat_axis=1, tiled=True
    )
    trained = [
        train_client(owned[i], tokens[i], labels[i], byte_full, out_full, products)
        for i in range(per_device)
    ]
    deltas = jnp.stack([t[0] for t in trained])
    losses = jnp.stack([t[1] for t in trained])
    returned = lax.all_to_all(deltas, "head", split_axis=1, concat_axis=0, tiled=True)
    received = lax.all_gather(returned, "client", axis=0, tiled=True)
    back = lax.dot_general(
        received, head_weight, (((1,), (1,)), ((), ())), preferred_element_type=jnp.float32
    )
    back = lax.all_to_all(
        back.reshape(head_count, rows // head_count, back.shape[1]), "head", split_axis=0, concat_axis=0
    )
    back = jnp.sum(back, 0)
    back = lax.all_to_all(
        jnp.broadcast_to(back[None], (head_count,) + back.shape), "head", split_axis=0, concat_axis=0
    )
    hidden_back = back.reshape(rows, back.shape[2])
    grad_sum = lax.dot_general(
        hidden, received, (((0,), (0,)), ((), ())), preferred_element_type=jnp.float32
    )
    masked = jnp.where(preact > 0, hidden_back, 0.0)
    in_grad = lax.dot_general(
        chosen.astype(jnp.float32),
        masked,
        (((0,), (0,)), ((), ())),
        precision=FULL,
    )
    return (grad_sum.astype(jnp.bfloat16), in_grad, losses)


def solution(mesh):
    placed = (
        P(),
        P(),
        P(None, "client"),
        P("client"),
        P("client", "head"),
        P(("head", "client"), None),
        P(("head", "client"), None),
        P(None, "client"),
        P(None, "client"),
    )
    return jax.shard_map(
        local,
        mesh=mesh,
        in_specs=placed,
        out_specs=(P("client", "head"), P(None, "client"), P(("head", "client"))),
        check_vma=False,
    )
```

time: 278 us -> 179 us (0.64); the launches traced: 274 us -> 178 us
  waiting for transfers between devices: 127 us -> 35.7 us
  matrix products: 95.1 us -> 68.6 us
  blocking collectives: 14.8 us -> 26.8 us
  starting transfers between devices: 5.69 us -> 13.2 us
    psum x1 -> x0, waiting for transfers between devices: 55.7 us -> none  [local(): hidden_back = lax.psum(hidden_back, 'head')]
    reduce_scatter x1 -> x0, waiting for transfers between devices: 32.6 us -> none  [local(): lax.psum_scatter(jnp.dot(hidden_rows, head_weight, preferred_element_type...]
    dot_general x17 -> x40, matrix products: 75.6 us -> 48.9 us  [the longest x1 15.3 us: local(): jnp.dot(hidden, head_weight, preferred_element_type=jnp.float32)]
    all_to_all x1 -> x3, waiting for transfers between devices: 0.01 us -> 19.1 us  [the longest x1 13.6 us: local(): lax.all_to_all(partial.reshape(group_count, rows // group_count, columns)...]
    all_gather x1, waiting for transfers between devices: 15.3 us -> 0.01 us  [local(): lax.all_gather(byte_table, 'client', axis=1, tiled=True)]
    all_to_all x0 -> x1, blocking collectives: none -> 14.9 us  [local(): lax.all_to_all(summed.astype(jnp.bfloat16), 'head', split_axis=0, concat_...]
    all_gather x1, waiting for transfers between devices: 7.8 us -> 0.02 us  [local(): lax.all_gather(out_table, 'client', axis=1, tiled=True)]
    all_to_all x1 -> x3, starting transfers between devices: 5.49 us -> 13.2 us  [the longest x1 5.51 us: local(): lax.all_to_all(back.reshape(head_count, rows // head_count, back.shape[1]...]
  transfers between devices with their start and end apart: 6 -> 6, of which waited for: 5 -> 3; matrix products, arithmetic and copies ran while one was open for 13% -> 25% of each run, Pallas kernels for 0% -> 0%
where the time goes in v1:
time: 179 us; the launch traced here: 178 us
  matrix products  68.6 us (38%)
  waiting for transfers between devices  35.7 us (20%)
  blocking collectives  26.8 us (15%)
  between operations  16.6 us (9%)
  starting transfers between devices  13.2 us (7%)
  local copies, waits for them, and re-layouts  13 us (7%)
  other arithmetic  4.36 us (2%)
    dot_general x1, matrix products, local(): lax.dot_general(received, head_weight, (((1,), (1,)), ((), ())), preferre...  17.2 us
    dot_general x1, matrix products, local(): jnp.dot(hidden, head_weight, preferred_element_type=jnp.float32)  15.3 us
    all_gather x1, waiting for transfers between devices, local(): received = lax.all_gather(returned, 'client', axis=0, tiled=True)  15.2 us
    all_to_all x1, blocking collectives, local(): lax.all_to_all(summed.astype(jnp.bfloat16), 'head', split_axis=0, concat_...  14.9 us
    dot_general x1, matrix products, local(): lax.dot_general(hidden, received, (((0,), (0,)), ((), ())), preferred_ele...  14.9 us
    all_to_all x1, waiting for transfers between devices, local(): lax.all_to_all(partial.reshape(group_count, rows // group_count, columns)...  13.6 us
    dot_general x12, matrix products, exact(): lax.dot_general(x, y, (((over_x,), (over_y,)), ((), ())), preferred_eleme...  12.7 us
    all_to_all x1, blocking collectives, local(): lax.all_to_all(deltas, 'head', split_axis=1, concat_axis=0, tiled=True)  11.9 us
  transfers between devices with their start and end apart: 6, of which 3 were waited for; matrix products, arithmetic and copies ran while one was open for 25% of the time, Pallas kernels for 0%

profile of v1, /device:TPU:0, one launch (start us, length us, event | category | flops | bytes accessed | tf_op | source)
XLA Modules:
  0.0 178.3 jit_solution(9570034128305382176)
XLA Ops:
  8.8 1.5 gather_fusion
  10.3 0.9 convolution_add_fusion.2
  11.2 15.3 %fusion = bf16[4,8,16384]{2,1,0:T(8,128)(2,1)} fusion(bf16[1024,16384]{1,0:T(8,128)(2,1)} %param.13, f32[32,1024]{1,0:T(8,128)S(1)} %convolution_add_fusion.2), kind=kOutput, calls=%fused_computation.3 | convolution fusion | flops 1074331648 | bytes 34734080 | tf_op jit(solution)/shard_map/dot_general | solution.py:129
  26.5 4.3 %all-to-all-start = ((bf16[4,8,16384]{2,1,0:T(8,128)(2,1)}), bf16[4,8,16384]{2,1,0:T(8,128)(2,1)S(1)}, u32[]{:S(2)}, u32[]{:S(2)}) async-start(bf16[4,8,16384]{2,1,0:T(8,128)(2,1)} %fusion), calls=%async_computation | async-start | bytes 2097152 | tf_op jit(solution)/shard_map/all_to_all | solution.py:131
  31.6 13.6 %all-to-all-done = bf16[4,8,16384]{2,1,0:T(8,128)(2,1)S(1)} async-done(((bf16[4,8,16384]{2,1,0:T(8,128)(2,1)}), bf16[4,8,16384]{2,1,0:T(8,128)(2,1)S(1)}, u32[]{:S(2)}, u32[]{:S(2)}) %all-to-all-start) | async-done | bytes 1048608 | tf_op jit(solution)/shard_map/all_to_all | solution.py:131
  47.0 14.9 %all_to_all.45 = bf16[8,2,8192]{2,1,0:T(2,128)(2,1)S(1)} all-to-all(bf16[8,2,8192]{2,1,0:T(2,128)(2,1)S(1)} %reshape.188), channel_id=1, replica_groups=mesh['head'=8,'client'=4] {'head'}, dimensions={0} | all-to-all | bytes 524288 | tf_op jit(solution)/shard_map/all_to_all | solution.py:135
  62.2 1.2 slice_reduce_fusion
  63.4 1.7 reshape.171
  65.4 3.1 %select_reduce_fusion = (f32[256]{0:T(256)S(1)}, f32[256,256]{0,1:T(8,128)S(1)}) fusion(bf16[256,4096]{1,0:T(8,128)(2,1)} %all-gather.5.cloned.1.call-done), kind=kOutput, calls=%fused_computation.58 | convolution fusion | flops 537067264 | bytes 2360320 | tf_op jit(solution)/shard_map/dot_general | solution.py:20
  70.2 2.4 %fusion.97 = f32[16,256]{1,0:T(8,128)S(1)} fusion(bf16[16,4096]{1,0:T(8,128)(2,1)S(1)} %reshape.172, bf16[256,4096]{1,0:T(8,128)(2,1)} %all-gather.7.cloned.1.call-done), kind=kOutput, calls=%fused_computation.165 | convolution fusion | flops 33554432 | bytes 2244608 | tf_op jit(solution)/shard_map/dot_general | solution.py:20
  73.8 0.9 multiply_reduce_fusion
  81.5 1.3 copy.19
  82.9 2.0 %reshape.173 = bf16[65536]{0:T(1024)(128)(2,1)S(1)} reshape(bf16[4096,16]{1,0:T(8,128)(2,1)} %copy.19) | data formatting | bytes 262144 | tf_op jit(solution)/shard_map/reshape | solution.py:110
  85.1 2.1 %fusion.42 = f32[32,4096]{1,0:T(8,128)S(1)} fusion(bf16[256,4096]{1,0:T(8,128)(2,1)} %all-gather.7.cloned.1.call-done, bf16[256,16]{0,1:T(8,128)(2,1)S(1)} %get-tuple-element.17, bf16[256,16]{0,1:T(8,128)(2,1)S(1)} %get-tuple-element.16), kind=kOutput, calls=%fused_computation.96 | convolution fusion | flops 67141632 | bytes 2637824 | tf_op jit(solution)/shard_map/dot_general | solution.py:20
  88.4 2.2 %reduce.7 = bf16[8,16384]{1,0:T(8,128)(2,1)S(1)} reduce(bf16[8,1,16384]{2,1,0:T(2,128)(2,1)S(1)} %bitcast.120, bf16[]{:T(256)} %broadcast.252), dimensions={1}, to_apply=%bitcast.52.reduce_sub_computation | reduce | bytes 524290
  90.8 11.9 %all_to_all.46 = bf16[8,2,8192]{2,1,0:T(2,128)(2,1)S(1)} all-to-all(bf16[8,2,8192]{2,1,0:T(2,128)(2,1)S(1)} %reshape.190), channel_id=1, replica_groups=mesh['head'=8,'client'=4] {'head'}, dimensions={0} | all-to-all | bytes 524288 | tf_op jit(solution)/shard_map/all_to_all | solution.py:144
  103.0 1.0 copy.21
  104.0 15.2 %all-gather.9.cloned.1.call-done = bf16[1,32,16384]{2,1,0:T(8,128)(2,1)} async-done(((bf16[1,8,16384]{2,1,0:T(8,128)(2,1)}), bf16[1,32,16384]{2,1,0:T(8,128)(2,1)}) %all-gather.9.cloned.1.call-update) | async-done | bytes 1048592 | tf_op jit(solution)/shard_map/all_gather | solution.py:145
  119.2 17.2 %fusion.11 = f32[32,1024]{1,0:T(8,128)S(1)} fusion(bf16[1024,16384]{1,0:T(8,128)(2,1)} %param.13, bf16[1,32,16384]{2,1,0:T(8,128)(2,1)} %all-gather.9.cloned.1.call-done), kind=kOutput, calls=%fused_computation.39 | convolution fusion | flops 1073741824 | bytes 34734080 | tf_op jit(solution)/shard_map/dot_general | solution.py:146
  137.1 5.5 %all-to-all-start.3 = ((f32[8,4,1024]{2,1,0:T(4,128)}), f32[8,4,1024]{2,1,0:T(4,128)S(1)}, u32[]{:S(2)}, u32[]{:S(2)}) async-start(f32[8,4,1024]{2,1,0:T(4,128)} %reshape.175), calls=%async_computation.3 | async-start | bytes 262144 | tf_op jit(solution)/shard_map/all_to_all | solution.py:149
  144.6 5.5 %all-to-all-done.3 = f32[8,4,1024]{2,1,0:T(4,128)S(1)} async-done(((f32[8,4,1024]{2,1,0:T(4,128)}), f32[8,4,1024]{2,1,0:T(4,128)S(1)}, u32[]{:S(2)}, u32[]{:S(2)}) %all-to-all-start.3) | async-done | bytes 131104 | tf_op jit(solution)/shard_map/all_to_all | solution.py:149
  150.7 3.4 %all-to-all-start.4 = ((f32[8,4,1024]{2,1,0:T(4,128)}), f32[8,4,1024]{2,1,0:T(4,128)S(1)}, u32[]{:S(2)}, u32[]{:S(2)}) async-start(f32[8,4,1024]{2,1,0:T(4,128)} %broadcast_in_dim.8), calls=%async_computation.4 | async-start | bytes 262144 | tf_op jit(solution)/shard_map/all_to_all | solution.py:153
  154.1 14.9 %convolution_convert_fusion = bf16[1024,16384]{1,0:T(8,128)(2,1)} fusion(bf16[1,32,16384]{2,1,0:T(8,128)(2,1)S(1)} %copy-done.4, f32[32,1024]{1,0:T(8,128)S(1)} %convolution_add_fusion.2), kind=kOutput, calls=%fused_computation.1 | convolution fusion | flops 1090584576 | bytes 34734080 | tf_op jit(solution)/shard_map/dot_general | solution.py:157
  169.1 1.6 fusion.24
  (90 shorter events, 18.2 us)
Async XLA Ops:
  7.2 3.1 %copy-start = (bf16[256,1024]{1,0:T(8,128)(2,1)S(1)}, bf16[256,1024]{1,0:T(8,128)(2,1)}, u32[]{:S(2)}) copy-start(bf16[256,1024]{1,0:T(8,128)(2,1)} %param.11) | copy-start | bytes 1572868
  7.2 58.2 %all-gather.5.cloned.1.call-start = ((), (), s32[]{:S(2)}) async-start(), calls=%async_computation.5 | async-start | bytes 2621440 | tf_op jit(solution)/shard_map/all_gather | solution.py:121
  26.5 18.7 %all-to-all-start = ((bf16[4,8,16384]{2,1,0:T(8,128)(2,1)}), bf16[4,8,16384]{2,1,0:T(8,128)(2,1)S(1)}, u32[]{:S(2)}, u32[]{:S(2)}) async-start(bf16[4,8,16384]{2,1,0:T(8,128)(2,1)} %fusion), calls=%async_computation | async-start | bytes 2097152 | tf_op jit(solution)/shard_map/all_to_all | solution.py:131
  30.8 39.4 %all-gather.7.cloned.1.call-start = ((), (), s32[]{:S(2)}) async-start(), calls=%async_computation.6 | async-start | bytes 2621440 | tf_op jit(solution)/shard_map/all_gather | solution.py:122
  31.5 87.7 %all-gather.9.cloned.1.call-start = ((), (), s32[]{:S(2)}) async-start(), calls=%async_computation.7 | async-start | bytes 1310720 | tf_op jit(solution)/shard_map/all_gather | solution.py:145
  65.3 3.2 %copy-start.2 = (bf16[256,4096]{1,0:T(8,128)(2,1)S(1)}, bf16[256,4096]{1,0:T(8,128)(2,1)}, u32[]{:S(2)}) copy-start(bf16[256,4096]{1,0:T(8,128)(2,1)} %all-gather.5.cloned.1.call-done) | copy-start | bytes 6291460
  65.3 3.2 %copy-start.5 = (bf16[4096,16]{1,0:T(8,128)(2,1)S(1)}, bf16[4096,16]{1,0:T(8,128)(2,1)}, u32[]{:S(2)}) copy-start(bf16[4096,16]{1,0:T(8,128)(2,1)} %reshape.171) | copy-start | bytes 393220
  70.1 2.4 %copy-start.3 = (bf16[256,4096]{1,0:T(8,128)(2,1)S(1)}, bf16[256,4096]{1,0:T(8,128)(2,1)}, u32[]{:S(2)}) copy-start(bf16[256,4096]{1,0:T(8,128)(2,1)} %all-gather.7.cloned.1.call-done) | copy-start | bytes 6291460
  72.5 1.2 copy-start.6
  72.6 1.2 copy-start.7
  119.2 34.9 %copy-start.4 = (bf16[1,32,16384]{2,1,0:T(8,128)(2,1)S(1)}, bf16[1,32,16384]{2,1,0:T(8,128)(2,1)}, u32[]{:S(2)}) copy-start(bf16[1,32,16384]{2,1,0:T(8,128)(2,1)} %all-gather.9.cloned.1.call-done) | copy-start | bytes 3145732
  137.1 12.9 %all-to-all-start.3 = ((f32[8,4,1024]{2,1,0:T(4,128)}), f32[8,4,1024]{2,1,0:T(4,128)S(1)}, u32[]{:S(2)}, u32[]{:S(2)}) async-start(f32[8,4,1024]{2,1,0:T(4,128)} %reshape.175), calls=%async_computation.3 | async-start | bytes 262144 | tf_op jit(solution)/shard_map/all_to_all | solution.py:149
  150.7 18.3 %all-to-all-start.4 = ((f32[8,4,1024]{2,1,0:T(4,128)}), f32[8,4,1024]{2,1,0:T(4,128)S(1)}, u32[]{:S(2)}, u32[]{:S(2)}) async-start(f32[8,4,1024]{2,1,0:T(4,128)} %broadcast_in_dim.8), calls=%async_computation.4 | async-start | bytes 262144 | tf_op jit(solution)/shard_map/all_to_all | solution.py:153
  154.1 16.5 %copy-start.1 = (bf16[256,1024]{1,0:T(8,128)(2,1)S(1)}, bf16[256,1024]{1,0:T(8,128)(2,1)}, u32[]{:S(2)}) copy-start(bf16[256,1024]{1,0:T(8,128)(2,1)} %param.11) | copy-start | bytes 1572868
Sparse Core Ops, SparseCore 0:
  9.5 25.2 all-gather.4
  36.4 22.5 all-gather.6
  104.2 15.0 all-gather.8
